TPU v7x, 128 devices: a whole 4x4x4 slice. The times are simulated.
128 devices in a mesh: rows: 32 (over x, z, core), cols: 4 (over y).
Axes of the slice: x: 4, y: 4, z: 4, core: 2. Of those that a mesh axis runs over, the one named last changes fastest.
Arguments:
- basis: float32 [262144, 256], P(('rows', 'cols')), may hold values from -8 to 8, as said below
- new_vectors: float32 [262144, 128], P(('rows', 'cols')), may hold values from -180 to 180
- jacobian: float32 [262144, 1024], P(('rows', 'cols')), may hold values from -0.1875 to 0.1875
Outputs:
- merged: float32 [262144, 384], P(('rows', 'cols'))
Inputs may be any that keep to these rules, and one draw needn't show every extreme that they name: The stored basis is orthonormal under the inner product divided by 262144 up to a drift of orthogonality: basis^T basis / 262144 differs from the identity by about 0.1 to 0.3 in spectral norm.
All inputs are finite; a program needn't handle non-finite values.
Results may differ from a plain program's by a relative error of at most 0.00005.
Values sent between devices are 32-bit elements; how exact they have to be, the bound alone decides.
A program may use at most 64 MiB of HBM per device.

v0:
```python
import functools

import jax
import jax.numpy as jnp
from jax import lax
from jax.experimental import pallas as pl
from jax.experimental.pallas import tpu as pltpu
from jax.sharding import PartitionSpec as P

SIDE = 4
STREAMS = 4
ORDERS = ((0, 1, 2), (1, 2, 0), (2, 0, 1), (0, 2, 1))
OFFSETS = (2, 1, 3)
ROWS = 1024


def sum_kernel(y_ref, out_ref, z0, r0, z1, r1, z2, r2, r3, s0, t0, s1, t1):
    row, col = lax.axis_index("rows"), lax.axis_index("cols")
    core = lax.rem(row, 2)
    place = (lax.div(row, 2 * SIDE), col, lax.rem(lax.div(row, 2), SIDE))

    def device(coords, which):
        return (coords[0] * (2 * SIDE) + coords[2] * 2 + which, coords[1])

    def peer(axis, offset):
        coords = list(place)
        coords[axis] = lax.rem(place[axis] + offset, SIDE)
        return coords

    partner = device(place, 1 - core)
    barrier = pltpu.get_barrier_semaphore()
    pl.semaphore_signal(barrier, inc=1, device_id=partner, device_id_type=pl.DeviceIdType.MESH)
    for axis in range(3):
        for offset in OFFSETS:
            pl.semaphore_signal(
                barrier, inc=1, device_id=device(peer(axis, offset), core), device_id_type=pl.DeviceIdType.MESH
            )
    pl.semaphore_wait(barrier, 1 + 3 * len(OFFSETS))

    sent = []

    def send(src, dst, send_sem, recv_sem, target):
        copy = pltpu.make_async_remote_copy(
            src_ref=src,
            dst_ref=dst,
            send_sem=send_sem,
            recv_sem=recv_sem,
            device_id=target,
            device_id_type=pl.DeviceIdType.MESH,
        )
        copy.start()
        sent.append(copy)
        return copy

    half = ROWS // 2
    order = (3, 0, 1, 2)
    mine = pl.multiple_of(core * half, half)
    other = pl.multiple_of((1 - core) * half, half)
    stage = {}
    for s in order:
        stage[s] = send(y_ref.at[s, pl.ds(other, half)], r0.at[s], s0.at[0, s], t0.at[0, s], partner)

    size = half
    parts = (r1, r2, r3)
    for phase in range(3):
        size //= SIDE
        nxt = {}
        for s in order:
            axis = ORDERS[s][phase]
            if phase == 0:
                stage[s].wait_recv()
                z0[s] = y_ref[s, pl.ds(mine, half)] + r0[s]
            else:
                for copy in stage[s]:
                    copy.wait_recv()
                before = ORDERS[s][phase - 1]
                prev, got = (z0, r1) if phase == 1 else (z1, r2)
                start = pl.multiple_of(place[before] * (size * SIDE), size * SIDE)
                dest = z1 if phase == 1 else z2
                dest[s] = prev[s, pl.ds(start, size * SIDE)] + got[s, 0] + got[s, 1] + got[s, 2]
            src = (z0, z1, z2)[phase]
            nxt[s] = []
            for slot, offset in enumerate(OFFSETS):
                coords = peer(axis, offset)
                start = pl.multiple_of(coords[axis] * size, size)
                nxt[s].append(
                    send(
                        src.at[s, pl.ds(start, size)],
                        parts[phase].at[s, slot],
                        s1.at[phase, s, slot],
                        t1.at[phase, s, slot],
                        device(coords, core),
                    )
                )
        stage = nxt

    for phase in range(3):
        back = 2 - phase
        nxt = {}
        for s in order:
            axis = ORDERS[s][back]
            for copy in stage[s]:
                copy.wait_recv()
            start = mine
            width = half
            for done in range(back + 1):
                width //= SIDE
                start = start + place[ORDERS[s][done]] * width
            start = pl.multiple_of(start, width)
            if phase == 0:
                own = pl.multiple_of(place[axis] * width, width)
                out_ref[s, pl.ds(start, width)] = z2[s, pl.ds(own, width)] + r3[s, 0] + r3[s, 1] + r3[s, 2]
            nxt[s] = []
            for slot, offset in enumerate(OFFSETS):
                nxt[s].append(
                    send(
                        out_ref.at[s, pl.ds(start, width)],
                        out_ref.at[s, pl.ds(start, width)],
                        s1.at[3 + phase, s, slot],
                        t1.at[3 + phase, s, slot],
                        device(peer(axis, offset), core),
                    )
                )
        stage = nxt
    last = []
    for s in order:
        for copy in stage[s]:
            copy.wait_recv()
        last.append(send(out_ref.at[s, pl.ds(mine, half)], out_ref.at[s, pl.ds(mine, half)], s0.at[1, s], t0.at[1, s], partner))
    for copy in last:
        copy.wait_recv()
    for copy in sent:
        copy.wait_send()


def sum_all(y):
    dma = pltpu.SemaphoreType.DMA
    half = ROWS // 2
    f32 = jnp.float32
    return pl.pallas_call(
        sum_kernel,
        out_shape=jax.ShapeDtypeStruct(y.shape, f32),
        in_specs=[pl.BlockSpec(memory_space=pltpu.VMEM)],
        out_specs=pl.BlockSpec(memory_space=pltpu.VMEM),
        scratch_shapes=[
            pltpu.VMEM((STREAMS, half, 128), f32),
            pltpu.VMEM((STREAMS, half, 128), f32),
            pltpu.VMEM((STREAMS, half // 4, 128), f32),
            pltpu.VMEM((STREAMS, 3, half // 4, 128), f32),
            pltpu.VMEM((STREAMS, half // 16, 128), f32),
            pltpu.VMEM((STREAMS, 3, half // 16, 128), f32),
            pltpu.VMEM((STREAMS, 3, half // 64, 128), f32),
            dma((2, STREAMS)),
            dma((2, STREAMS)),
            dma((6, STREAMS, 3)),
            dma((6, STREAMS, 3)),
        ],
        compiler_params=pltpu.CompilerParams(collective_id=0, has_side_effects=True, vmem_limit_bytes=20 * 1024 * 1024),
        name="sum_all",
    )(y)


def mat(left, right, precision=lax.Precision.HIGHEST):
    return jnp.dot(left, right, precision=precision, preferred_element_type=jnp.float32)


def tmat(left, right, precision=lax.Precision.HIGHEST):
    return lax.dot_general(
        left,
        right,
        (((0,), (0,)), ((), ())),
        precision=precision,
        preferred_element_type=jnp.float32,
    )


LEAF = 16
PIECES = 8


def split3(value):
    high = value.astype(jnp.bfloat16)
    rest = value - high.astype(jnp.float32)
    middle = rest.astype(jnp.bfloat16)
    low = (rest - middle.astype(jnp.float32)).astype(jnp.bfloat16)
    return high, middle, low


def split2(value):
    high = value.astype(jnp.bfloat16)
    return high, (value - high.astype(jnp.float32)).astype(jnp.bfloat16)


def nt(left, right):
    return lax.dot_general(left, right, (((1,), (1,)), ((), ())), preferred_element_type=jnp.float32)


def build(y_ref, scale):
    cut = {}
    at = 0
    for i in range(3):
        for j in range(i + 1):
            cut[i, j] = y_ref[3, at : at + 128] * scale
            at += 128
    s_vv = jnp.concatenate(
        [jnp.concatenate([cut[0, 0], cut[1, 0].T], axis=1), jnp.concatenate([cut[1, 0], cut[1, 1]], axis=1)], axis=0
    )
    s_vw = jnp.concatenate([cut[2, 0].T, cut[2, 1].T], axis=0)
    summed = s_vw + (s_vw - mat(s_vv, s_vw))
    cross = tmat(summed, s_vw)
    last = cut[2, 2] - cross - cross.T + tmat(summed, mat(s_vv, summed) + summed)
    hess = jnp.zeros((384, 384), jnp.float32)
    for pair in range(0, 8, 2):
        rows = [
            jnp.concatenate([y_ref[s, 128 * t : 128 * (t + 1)] for s in range(3)], axis=0) for t in (pair, pair + 1)
        ]
        high, low = split2(jnp.concatenate(rows, axis=1))
        hess = hess + (nt(high, low) + nt(low, high) + nt(high, high))
    hess = hess * scale
    ident = jnp.where(
        lax.broadcasted_iota(jnp.int32, (256, 256), 0) == lax.broadcasted_iota(jnp.int32, (256, 256), 1), 1.0, 0.0
    ).astype(jnp.float32)
    top = jnp.concatenate([ident, summed], axis=1)
    low = jnp.concatenate([summed.T, last], axis=1)
    return jnp.concatenate([top, low], axis=0) + hess


def leaf_step(a, block, step):
    tiles = LEAF // 8
    width = a.shape[1]
    first = pl.multiple_of(block * 128 + step * LEAF, LEAF)
    base = pl.multiple_of(block * 128, 128)
    sub = lax.broadcasted_iota(jnp.int32, (8, 128), 0)
    lane = lax.broadcasted_iota(jnp.int32, (8, 128), 1)
    columns = {}
    for t in range(tiles):
        diag = a[pl.ds(first + 8 * t, 8), pl.ds(base, 128)]
        for k in range(min(LEAF, 8 * (t + 1))):
            at = step * LEAF + k
            columns[k, t] = jnp.broadcast_to(diag[:, at : at + 1], (8, 128))
    panel = {}
    for t in range(tiles):
        for c in range(width // 128):
            place = lane + (128 * c - first)
            own = (place >= 0) & (place < LEAF)
            unit = jnp.where(place == sub + 8 * t, 1.0, 0.0)
            panel[t, c] = jnp.where(own, unit, a[pl.ds(first + 8 * t, 8), 128 * c : 128 * (c + 1)])
    factor = [jnp.zeros((8, 128), jnp.float32) for _ in range(tiles)]
    for j in range(LEAF):
        home, row = j // 8, j % 8
        pivot = jnp.broadcast_to(columns[j, home][row : row + 1], (8, 128))
        root = lax.rsqrt(pivot)
        inverse = root * root
        factor[home] = jnp.where(sub == row, root, factor[home])
        if j + 1 == LEAF:
            break
        mult = {}
        for t in range(home, tiles):
            value = columns[j, t] * inverse
            if t == home:
                value = jnp.where(sub > row, value, 0.0)
            mult[t] = value
        for k in range(j + 1, LEAF):
            spread = jnp.broadcast_to(columns[j, k // 8][k % 8 : k % 8 + 1], (8, 128))
            for t in range(k // 8, tiles):
                if k == j + 1:
                    columns[k, t] = columns[k, t] - (columns[j, t] * spread) * inverse
                else:
                    columns[k, t] = columns[k, t] - mult[t] * spread
        for c in range(width // 128):
            spread = jnp.broadcast_to(panel[home, c][row : row + 1], (8, 128))
            for t in range(home, tiles):
                panel[t, c] = panel[t, c] - mult[t] * spread
    rows = jnp.concatenate(
        [
            jnp.concatenate([panel[t, c] * factor[t] for c in range(width // 128)], axis=1)
            for t in range(tiles)
        ],
        axis=0,
    )
    place = lax.broadcasted_iota(jnp.int32, (LEAF, width), 1) - first
    right = split3(rows)
    left = split3(jnp.where(place >= LEAF, rows, 0.0))
    none = jnp.zeros((LEAF, width), jnp.bfloat16)
    pick = lambda parts, order: jnp.concatenate([parts[i] for i in order] + [none] * (PIECES - len(order)), axis=0)
    update = lax.dot_general(
        pick(left, (0, 0, 1, 0, 2, 1)),
        pick(right, (0, 1, 0, 2, 0, 1)),
        (((0,), (0,)), ((), ())),
        preferred_element_type=jnp.float32,
    )
    place = lax.broadcasted_iota(jnp.int32, (width, width), 1) - first
    own = (place >= 0) & (place < LEAF)
    a[...] = jnp.where(own, 0.0, a[...]) - update
    a[pl.ds(first, LEAF), :] = rows


def factor_kernel(scale, y_ref, a):
    a[...] = build(y_ref, scale)

    def block_step(block, _):
        for step in range(128 // LEAF):
            leaf_step(a, block, step)
        return 0

    lax.fori_loop(0, a.shape[0] // 128, block_step, 0)


def factor_inverse(summed, scale):
    return pl.pallas_call(
        functools.partial(factor_kernel, scale),
        out_shape=jax.ShapeDtypeStruct((384, 384), jnp.float32),
        in_specs=[pl.BlockSpec(memory_space=pltpu.VMEM)],
        out_specs=pl.BlockSpec(memory_space=pltpu.VMEM),
        compiler_params=pltpu.CompilerParams(vmem_limit_bytes=32 * 1024 * 1024),
        name="factor_inverse",
    )(summed)


def local(basis, new_vectors, jacobian):
    total = basis.shape[0] * lax.axis_size("rows") * lax.axis_size("cols")
    scale = 1.0 / total
    width = basis.shape[1]
    stacked = jnp.concatenate([basis, new_vectors], axis=1)
    full = tmat(stacked, stacked, lax.Precision.HIGH)
    proj = tmat(stacked, jacobian, lax.Precision.HIGH)
    width = basis.shape[1]
    parts = proj.reshape(3, 128, 8, 128).transpose(0, 2, 1, 3).reshape(3, ROWS, 128)
    cuts = [full[128 * i : 128 * (i + 1), 128 * j : 128 * (j + 1)] for i in range(3) for j in range(i + 1)]
    packed = jnp.concatenate(cuts + [jnp.zeros((ROWS - 768, 128), jnp.float32)], axis=0)
    summed = sum_all(jnp.concatenate([parts, packed[None]], axis=0))
    inverse = factor_inverse(summed, scale)
    return lax.dot_general(
        stacked,
        inverse,
        (((1,), (1,)), ((), ())),
        precision=lax.Precision.HIGH,
        preferred_element_type=jnp.float32,
    )


def solution(mesh):
    placed = (P(("rows", "cols"), None), P(("rows", "cols"), None), P(("rows", "cols"), None))
    return jax.shard_map(
        local, mesh=mesh, in_specs=placed, out_specs=P(("rows", "cols"), None), check_vma=False
    )
```

profile of v0, /device:TPU:1, one launch (start us, length us, event | category | flops | bytes accessed | tf_op | source)
XLA Modules:
  0.0 72.8 jit_solution(2154397569836982949)
XLA Ops:
  0.0 0.0 copy-start.1
  0.0 1.8 %constant_dynamic-update-slice_fusion.1 = f32[2048,384]{1,0:T(8,128)S(1)} fusion(f32[2048,256]{1,0:T(8,128)} %param.3), kind=kLoop, calls=%fused_computation.9 | loop fusion | bytes 4194304
  1.8 0.0 copy-done.1
  1.9 0.0 copy-start
  1.9 0.1 constant_dynamic-update-slice_fusion
  1.9 2.6 %fusion = f32[384,384]{1,0:T(8,128)S(1)} fusion(f32[2048,384]{1,0:T(8,128)S(1)} %constant_dynamic-update-slice_fusion), kind=kOutput, calls=%fused_computation.10 | convolution fusion | flops 1811939328 | bytes 3735552 | tf_op jit(solution)/shard_map/dot_general | solution.py:168
  4.7 0.6 copy-done
  5.2 5.8 %convolution_bitcast_fusion = f32[48,8,8,128]{3,1,2,0:T(8,128)S(1)} fusion(f32[2048,384]{1,0:T(8,128)S(1)} %constant_dynamic-update-slice_fusion, f32[2048,1024]{1,0:T(8,128)S(1)} %copy-done), kind=kOutput, calls=%fused_computation.1 | convolution fusion | flops 4831838208 | bytes 13107200 | tf_op jit(solution)/shard_map/dot_general | solution.py:168
  11.1 0.3 copy.5
  11.4 0.3 copy.4
  11.7 0.1 pad_maximum_fusion.y_ref
  11.9 39.7 %sum_all.1.y_ref = f32[4,1024,128]{2,1,0:T(8,128)S(1)} custom-call(f32[4,1024,128]{2,1,0:T(8,128)S(1)} %pad_maximum_fusion.y_ref), custom_call_target="tpu_custom_call" | custom-call | tf_op jit(solution)/shard_map/sum_all/pallas_call | solution.py:140
  51.6 16.5 %factor_inverse.1 = f32[384,384]{1,0:T(8,128)S(1)} custom-call(f32[4,1024,128]{2,1,0:T(8,128)S(1)} %sum_all.1.y_ref), custom_call_target="tpu_custom_call" | custom-call | tf_op jit(solution)/shard_map/factor_inverse/pallas_call | solution.py:310
  68.1 4.7 %fusion.1 = f32[2048,384]{1,0:T(8,128)} fusion(f32[2048,384]{1,0:T(8,128)S(1)} %constant_dynamic-update-slice_fusion, f32[384,384]{1,0:T(8,128)S(1)} %factor_inverse.1), kind=kOutput, calls=%fused_computation.11 | convolution fusion | flops 1811939328 | bytes 6881280 | tf_op jit(solution)/shard_map/dot_general | solution.py:333
  (6 shorter events, 0.1 us)
Async XLA Ops:
  0.0 1.9 %copy-start.1 = (f32[2048,128]{1,0:T(8,128)S(1)}, f32[2048,128]{1,0:T(8,128)}, u32[]{:S(2)}) copy-start(f32[2048,128]{1,0:T(8,128)} %param.4) | copy-start | bytes 3145732
  1.9 3.4 %copy-start = (f32[2048,1024]{1,0:T(8,128)S(1)}, f32[2048,1024]{1,0:T(8,128)}, u32[]{:S(2)}) copy-start(f32[2048,1024]{1,0:T(8,128)} %param.5) | copy-start | bytes 25165828
where the time goes:
time: 72.9 us; the launch traced here: 72.8 us
  Pallas kernels  56.2 us (77%)
  matrix products  13.2 us (18%)
  local copies, waits for them, and re-layouts  3.14 us (4%)
    pallas_call x1, Pallas kernels, sum_all(): pl.pallas_call(sum_kernel, out_shape=jax.ShapeDtypeStruct(y.shape, f32),...  39.7 us
    pallas_call x1, Pallas kernels, factor_inverse(): pl.pallas_call(functools.partial(factor_kernel, scale), out_shape=jax.Sha...  16.5 us
    dot_general x2, matrix products, tmat(): lax.dot_general(left, right, (((0,), (0,)), ((), ())), precision=precisio...  8.49 us
    dot_general x1, matrix products, local(): lax.dot_general(stacked, inverse, (((1,), (1,)), ((), ())), precision=lax...  4.69 us
    unnamed x11, local copies, waits for them, and re-layouts  2.79 us

commit v1 on v0

v1 whole, which is shorter than its diff:
```python
import functools

import jax
import jax.numpy as jnp
from jax import lax
from jax.experimental import pallas as pl
from jax.experimental.pallas import tpu as pltpu
from jax.sharding import PartitionSpec as P

SIDE = 4
STREAMS = 4
AXIS = (0, 1, 2, 0)
OFFSETS = (2, 1, 3, 0)
PLANE = sorted(
    [(b, c) for b in range(SIDE) for c in range(SIDE) if b or c],
    key=lambda at: -(min(at[0], SIDE - at[0]) + min(at[1], SIDE - at[1])),
)
ROWS = 1024
HALF = ROWS // 2
PART = HALF // SIDE
PIECE = PART // SIDE**2
ORDER = (3, 0, 1, 2)


class Links:
    def __init__(self):
        row, col = lax.axis_index("rows"), lax.axis_index("cols")
        self.core = lax.rem(row, 2)
        self.place = (lax.div(row, 2 * SIDE), col, lax.rem(lax.div(row, 2), SIDE))
        self.partner = self.device(self.place, 1 - self.core)
        self.sent = []

    def device(self, coords, which):
        return (coords[0] * (2 * SIDE) + coords[2] * 2 + which, coords[1])

    def moved(self, axes, offsets):
        coords = list(self.place)
        for axis, offset in zip(axes, offsets):
            coords[axis] = lax.rem(self.place[axis] + offset, SIDE)
        return coords

    def greet(self):
        barrier = pltpu.get_barrier_semaphore()
        others = [self.partner]
        for axis in range(3):
            others += [self.device(self.moved((axis,), (offset,)), self.core) for offset in OFFSETS[:3]]
        for axes in ((1, 2), (0, 2), (0, 1)):
            others += [self.device(self.moved(axes, at), self.core) for at in PLANE if at[0] and at[1]]
        for other in others:
            pl.semaphore_signal(barrier, inc=1, device_id=other, device_id_type=pl.DeviceIdType.MESH)
        self.greeted = (barrier, len(others))

    def meet(self):
        pl.semaphore_wait(*self.greeted)

    def send(self, src, dst, sems, at, target):
        copy = pltpu.make_async_remote_copy(
            src_ref=src,
            dst_ref=dst,
            send_sem=sems[0].at[at],
            recv_sem=sems[1].at[at],
            device_id=target,
            device_id_type=pl.DeviceIdType.MESH,
        )
        copy.start()
        self.sent.append(copy)
        return copy


def plane_of(s):
    return tuple(axis for axis in range(3) if axis != AXIS[s])


def share_core(links, s, y_ref, r0, sems):
    copies = []
    for slot, offset in enumerate(OFFSETS):
        at = links.moved((AXIS[s],), (offset,))[AXIS[s]] * PART
        rows = pl.ds(pl.multiple_of((1 - links.core) * HALF + at, PART), PART)
        keep = pl.ds(pl.multiple_of(at, PART), PART)
        copies.append(links.send(y_ref.at[s, rows], r0.at[s, keep], sems, (s, slot), links.partner))
    return copies


def share_line(links, s, waits, y_ref, r0, z0, r1, sems):
    copies = []
    for slot, offset in enumerate(OFFSETS):
        coords = links.moved((AXIS[s],), (offset,))
        at = coords[AXIS[s]] * PART
        rows = pl.ds(pl.multiple_of(links.core * HALF + at, PART), PART)
        keep = pl.ds(pl.multiple_of(at, PART), PART)
        waits[slot].wait_recv()
        z0[s, slot] = y_ref[s, rows] + r0[s, keep]
        if offset:
            copies.append(links.send(z0.at[s, slot], r1.at[s, slot], sems, (s, slot), links.device(coords, links.core)))
    return copies


def share_plane(links, s, waits, z0, r1, z1, r2, sems):
    for copy in waits:
        copy.wait_recv()
    z1[s] = (z0[s, 3] + r1[s, 0]) + (r1[s, 1] + r1[s, 2])
    copies = []
    axes = plane_of(s)
    for slot, offsets in enumerate(PLANE):
        coords = links.moved(axes, offsets)
        at = pl.multiple_of((coords[axes[0]] * SIDE + coords[axes[1]]) * PIECE, PIECE)
        copies.append(
            links.send(z1.at[s, pl.ds(at, PIECE)], r2.at[s, slot], sems, (s, slot), links.device(coords, links.core))
        )
    return copies


def spread_plane(links, s, waits, z1, r2, out_ref, sems):
    for copy in waits:
        copy.wait_recv()
    axes = plane_of(s)
    at = (links.place[axes[0]] * SIDE + links.place[axes[1]]) * PIECE
    parts = [z1[s, pl.ds(pl.multiple_of(at, PIECE), PIECE)]] + [r2[s, slot] for slot in range(len(PLANE))]
    while len(parts) > 1:
        parts = [left + right for left, right in zip(parts[::2], parts[1::2])]
    rows = pl.ds(pl.multiple_of(links.core * HALF + links.place[AXIS[s]] * PART + at, PIECE), PIECE)
    out_ref[s, rows] = parts[0]
    return [
        links.send(
            out_ref.at[s, rows],
            out_ref.at[s, rows],
            sems,
            (s, slot),
            links.device(links.moved(axes, offsets), links.core),
        )
        for slot, offsets in enumerate(PLANE)
    ]


def spread_line(links, s, waits, out_ref, sems, core_sems):
    for copy in waits:
        copy.wait_recv()
    rows = pl.ds(pl.multiple_of(links.core * HALF + links.place[AXIS[s]] * PART, PART), PART)
    block = out_ref.at[s, rows]
    copies = [
        links.send(block, block, sems, (s, slot), links.device(links.moved((AXIS[s],), (offset,)), links.core))
        for slot, offset in enumerate(OFFSETS[:3])
    ]
    return copies, [links.send(block, block, core_sems, (s, 3), links.partner)]


def spread_core(links, s, waits, out_ref, core_sems):
    copies = []
    for slot in (1, 2, 0):
        waits[slot].wait_recv()
        at = links.moved((AXIS[s],), (SIDE - OFFSETS[slot],))[AXIS[s]] * PART
        block = out_ref.at[s, pl.ds(pl.multiple_of(links.core * HALF + at, PART), PART)]
        copies.append(links.send(block, block, core_sems, (s, slot), links.partner))
    return copies


def split3(value):
    high = value.astype(jnp.bfloat16)
    rest = value - high.astype(jnp.float32)
    middle = rest.astype(jnp.bfloat16)
    low = (rest - middle.astype(jnp.float32)).astype(jnp.bfloat16)
    return high, middle, low


def split2(value):
    high = value.astype(jnp.bfloat16)
    return high, (value - high.astype(jnp.float32)).astype(jnp.bfloat16)


CHUNK = 512


def mm(left, right):
    return jnp.dot(left, right, preferred_element_type=jnp.float32)


def gram_and_project(v_ref, w_ref, j_ref, out_ref, s_buf, j_buf, high_t, low_t, g_acc, y_ref, z0, r0, r1, z1, r2, in_s, in_j, *sems):
    sems = [sems[i : i + 2] for i in range(0, 12, 2)]
    links = Links()
    links.greet()
    width, block = v_ref.shape[1], w_ref.shape[1]
    joint = width + block
    chunks = v_ref.shape[0] // CHUNK
    sides = [pl.multiple_of(which * HALF, HALF) for which in (1 - links.core, links.core)]

    def load_s(k):
        rows = pl.ds(pl.multiple_of(k * CHUNK, CHUNK), CHUNK)
        return (
            pltpu.make_async_copy(v_ref.at[rows], s_buf.at[rows, pl.ds(0, width)], in_s.at[0, k]),
            pltpu.make_async_copy(w_ref.at[rows], s_buf.at[rows, pl.ds(width, block)], in_s.at[1, k]),
        )

    def load_j(side, k):
        rows = pl.ds(pl.multiple_of(k * CHUNK, CHUNK), CHUNK)
        return pltpu.make_async_copy(j_ref.at[rows, pl.ds(sides[side], HALF)], j_buf.at[side, rows], in_j.at[side, k])

    for k in range(chunks):
        for copy in load_s(k):
            copy.start()
    for side in range(2):
        for k in range(chunks):
            load_j(side, k).start()
    g_acc[...] = jnp.zeros_like(g_acc)
    y_ref[...] = jnp.zeros_like(y_ref)

    def gram_step(k, _):
        for copy in load_s(k):
            copy.wait()
        rows = pl.ds(pl.multiple_of(k * CHUNK, CHUNK), CHUNK)
        value = s_buf[rows]
        flipped = split2(value.T)
        high_t[:, rows], low_t[:, rows] = flipped
        g_acc[...] += mm(flipped[0], jnp.concatenate(split2(value), axis=1))
        return 0

    lax.fori_loop(0, chunks, gram_step, 0)
    at = 0
    for i in range(3):
        for j in range(i + 1):
            tile = g_acc[128 * i : 128 * (i + 1), 128 * j : 128 * (j + 1)]
            mixed = g_acc[128 * i : 128 * (i + 1), joint + 128 * j : joint + 128 * (j + 1)]
            other = g_acc[128 * j : 128 * (j + 1), joint + 128 * i : joint + 128 * (i + 1)]
            y_ref[3, at : at + 128] = tile + (mixed + other.T)
            at += 128

    def project(side):
        def step(k, _):
            load_j(side, k).wait()
            rows = pl.ds(pl.multiple_of(k * CHUNK, CHUNK), CHUNK)
            high, low = split2(j_buf[side, rows])
            lead = high_t[:, rows]
            value = mm(lead, low) + mm(low_t[:, rows], high) + mm(lead, high)
            for s in range(3):
                for t in range(SIDE):
                    at = pl.ds(pl.multiple_of(sides[side] + 128 * t, 128), 128)
                    y_ref[s, at] += value[128 * s : 128 * (s + 1), 128 * t : 128 * (t + 1)]
            return 0

        lax.fori_loop(0, chunks, step, 0)

    links.meet()
    stage = {3: share_core(links, 3, y_ref, r0, sems[0])}
    project(0)
    for s in range(3):
        stage[s] = share_core(links, s, y_ref, r0, sems[0])
    stage[3] = share_line(links, 3, stage[3], y_ref, r0, z0, r1, sems[1])
    project(1)
    stage[3] = share_plane(links, 3, stage[3], z0, r1, z1, r2, sems[2])
    for s in range(3):
        stage[s] = share_line(links, s, stage[s], y_ref, r0, z0, r1, sems[1])
    stage[3] = spread_plane(links, 3, stage[3], z1, r2, out_ref, sems[3])
    for s in range(3):
        stage[s] = share_plane(links, s, stage[s], z0, r1, z1, r2, sems[2])
    last = []
    stage[3], own = spread_line(links, 3, stage[3], out_ref, sems[4], sems[5])
    last += own
    for s in range(3):
        stage[s] = spread_plane(links, s, stage[s], z1, r2, out_ref, sems[3])
    last += spread_core(links, 3, stage[3], out_ref, sems[5])
    for s in range(3):
        stage[s], own = spread_line(links, s, stage[s], out_ref, sems[4], sems[5])
        last += own
    for s in range(3):
        last += spread_core(links, s, stage[s], out_ref, sems[5])
    for copy in last:
        copy.wait_recv()
    for copy in links.sent:
        copy.wait_send()


def summed_products(basis, new_vectors, jacobian):
    f32, bf16, dma = jnp.float32, jnp.bfloat16, pltpu.SemaphoreType.DMA
    rows = basis.shape[0]
    joint = basis.shape[1] + new_vectors.shape[1]
    sems = []
    for count in (4, 3, len(PLANE), len(PLANE), 3, 4):
        sems += [dma((STREAMS, count))] * 2
    return pl.pallas_call(
        gram_and_project,
        out_shape=jax.ShapeDtypeStruct((STREAMS, ROWS, 128), f32),
        in_specs=[pl.BlockSpec(memory_space=pltpu.HBM)] * 3,
        out_specs=pl.BlockSpec(memory_space=pltpu.VMEM),
        scratch_shapes=[
            pltpu.VMEM((rows, joint), f32),
            pltpu.VMEM((2, rows, HALF), f32),
            pltpu.VMEM((joint, rows), bf16),
            pltpu.VMEM((joint, rows), bf16),
            pltpu.VMEM((joint, 2 * joint), f32),
            pltpu.VMEM((STREAMS, ROWS, 128), f32),
            pltpu.VMEM((STREAMS, SIDE, PART, 128), f32),
            pltpu.VMEM((STREAMS, HALF, 128), f32),
            pltpu.VMEM((STREAMS, 3, PART, 128), f32),
            pltpu.VMEM((STREAMS, PART, 128), f32),
            pltpu.VMEM((STREAMS, len(PLANE), PIECE, 128), f32),
            dma((2, rows // CHUNK)),
            dma((2, rows // CHUNK)),
        ]
        + sems,
        compiler_params=pltpu.CompilerParams(
            collective_id=0, has_side_effects=True, vmem_limit_bytes=48 * 1024 * 1024
        ),
        name="summed_products",
    )(basis, new_vectors, jacobian)


def mat(left, right, precision=lax.Precision.HIGHEST):
    return jnp.dot(left, right, precision=precision, preferred_element_type=jnp.float32)


def tmat(left, right, precision=lax.Precision.HIGHEST):
    return lax.dot_general(
        left,
        right,
        (((0,), (0,)), ((), ())),
        precision=precision,
        preferred_element_type=jnp.float32,
    )


LEAF = 16
PIECES = 8


def nt(left, right):
    return lax.dot_general(left, right, (((1,), (1,)), ((), ())), preferred_element_type=jnp.float32)


def build(y_ref, scale):
    cut = {}
    at = 0
    for i in range(3):
        for j in range(i + 1):
            cut[i, j] = y_ref[3, at : at + 128] * scale
            at += 128
    s_vv = jnp.concatenate(
        [jnp.concatenate([cut[0, 0], cut[1, 0].T], axis=1), jnp.concatenate([cut[1, 0], cut[1, 1]], axis=1)], axis=0
    )
    s_vw = jnp.concatenate([cut[2, 0].T, cut[2, 1].T], axis=0)
    summed = s_vw + (s_vw - mat(s_vv, s_vw))
    cross = tmat(summed, s_vw)
    last = cut[2, 2] - cross - cross.T + tmat(summed, mat(s_vv, summed) + summed)
    hess = jnp.zeros((384, 384), jnp.float32)
    for pair in range(0, 8, 2):
        rows = [
            jnp.concatenate([y_ref[s, 128 * t : 128 * (t + 1)] for s in range(3)], axis=0) for t in (pair, pair + 1)
        ]
        high, low = split2(jnp.concatenate(rows, axis=1))
        hess = hess + (nt(high, low) + nt(low, high) + nt(high, high))
    hess = hess * scale
    ident = jnp.where(
        lax.broadcasted_iota(jnp.int32, (256, 256), 0) == lax.broadcasted_iota(jnp.int32, (256, 256), 1), 1.0, 0.0
    ).astype(jnp.float32)
    top = jnp.concatenate([ident, summed], axis=1)
    low = jnp.concatenate([summed.T, last], axis=1)
    return jnp.concatenate([top, low], axis=0) + hess


def leaf_step(a, block, step):
    tiles = LEAF // 8
    width = a.shape[1]
    first = pl.multiple_of(block * 128 + step * LEAF, LEAF)
    base = pl.multiple_of(block * 128, 128)
    sub = lax.broadcasted_iota(jnp.int32, (8, 128), 0)
    lane = lax.broadcasted_iota(jnp.int32, (8, 128), 1)
    columns = {}
    for t in range(tiles):
        diag = a[pl.ds(first + 8 * t, 8), pl.ds(base, 128)]
        for k in range(min(LEAF, 8 * (t + 1))):
            at = step * LEAF + k
            columns[k, t] = jnp.broadcast_to(diag[:, at : at + 1], (8, 128))
    panel = {}
    for t in range(tiles):
        for c in range(width // 128):
            place = lane + (128 * c - first)
            own = (place >= 0) & (place < LEAF)
            unit = jnp.where(place == sub + 8 * t, 1.0, 0.0)
            panel[t, c] = jnp.where(own, unit, a[pl.ds(first + 8 * t, 8), 128 * c : 128 * (c + 1)])
    factor = [jnp.zeros((8, 128), jnp.float32) for _ in range(tiles)]
    for j in range(LEAF):
        home, row = j // 8, j % 8
        pivot = jnp.broadcast_to(columns[j, home][row : row + 1], (8, 128))
        root = lax.rsqrt(pivot)
        inverse = root * root
        factor[home] = jnp.where(sub == row, root, factor[home])
        if j + 1 == LEAF:
            break
        mult = {}
        for t in range(home, tiles):
            value = columns[j, t] * inverse
            if t == home:
                value = jnp.where(sub > row, value, 0.0)
            mult[t] = value
        for k in range(j + 1, LEAF):
            spread = jnp.broadcast_to(columns[j, k // 8][k % 8 : k % 8 + 1], (8, 128))
            for t in range(k // 8, tiles):
                if k == j + 1:
                    columns[k, t] = columns[k, t] - (columns[j, t] * spread) * inverse
                else:
                    columns[k, t] = columns[k, t] - mult[t] * spread
        for c in range(width // 128):
            spread = jnp.broadcast_to(panel[home, c][row : row + 1], (8, 128))
            for t in range(home, tiles):
                panel[t, c] = panel[t, c] - mult[t] * spread
    rows = jnp.concatenate(
        [
            jnp.concatenate([panel[t, c] * factor[t] for c in range(width // 128)], axis=1)
            for t in range(tiles)
        ],
        axis=0,
    )
    place = lax.broadcasted_iota(jnp.int32, (LEAF, width), 1) - first
    right = split3(rows)
    left = split3(jnp.where(place >= LEAF, rows, 0.0))
    none = jnp.zeros((LEAF, width), jnp.bfloat16)
    pick = lambda parts, order: jnp.concatenate([parts[i] for i in order] + [none] * (PIECES - len(order)), axis=0)
    update = lax.dot_general(
        pick(left, (0, 0, 1, 0, 2, 1)),
        pick(right, (0, 1, 0, 2, 0, 1)),
        (((0,), (0,)), ((), ())),
        preferred_element_type=jnp.float32,
    )
    place = lax.broadcasted_iota(jnp.int32, (width, width), 1) - first
    own = (place >= 0) & (place < LEAF)
    a[...] = jnp.where(own, 0.0, a[...]) - update
    a[pl.ds(first, LEAF), :] = rows


def factor_kernel(scale, y_ref, a):
    a[...] = build(y_ref, scale)

    def block_step(block, _):
        for step in range(128 // LEAF):
            leaf_step(a, block, step)
        return 0

    lax.fori_loop(0, a.shape[0] // 128, block_step, 0)


def factor_inverse(summed, scale):
    return pl.pallas_call(
        functools.partial(factor_kernel, scale),
        out_shape=jax.ShapeDtypeStruct((384, 384), jnp.float32),
        in_specs=[pl.BlockSpec(memory_space=pltpu.VMEM)],
        out_specs=pl.BlockSpec(memory_space=pltpu.VMEM),
        compiler_params=pltpu.CompilerParams(vmem_limit_bytes=32 * 1024 * 1024),
        name="factor_inverse",
    )(summed)


def local(basis, new_vectors, jacobian):
    total = basis.shape[0] * lax.axis_size("rows") * lax.axis_size("cols")
    scale = 1.0 / total
    stacked = jnp.concatenate([basis, new_vectors], axis=1)
    summed = summed_products(basis, new_vectors, jacobian)
    inverse = factor_inverse(summed, scale)
    return lax.dot_general(
        stacked,
        inverse,
        (((1,), (1,)), ((), ())),
        precision=lax.Precision.HIGH,
        preferred_element_type=jnp.float32,
    )


def solution(mesh):
    placed = (P(("rows", "cols"), None), P(("rows", "cols"), None), P(("rows", "cols"), None))
    return jax.shard_map(
        local, mesh=mesh, in_specs=placed, out_specs=P(("rows", "cols"), None), check_vma=False
    )
```

time: 72.9 us -> 68.1 us (0.934)
  matrix products: 13.2 us -> 4.69 us
  Pallas kernels: 56.2 us -> 60.4 us
    dot_general x2 -> x0, matrix products: 8.49 us -> none  [tmat(): lax.dot_general(left, right, (((0,), (0,)), ((), ())), precision=precisio...]
    pallas_call x1, Pallas kernels: 39.7 us -> 44 us  [summed_products(): pl.pallas_call(gram_and_project, out_shape=jax.ShapeDtypeStruct((STREAMS,...]
    unnamed x11 -> x4, local copies, waits for them, and re-layouts: 2.79 us -> 2.81 us
where the time goes in v1:
time: 68.1 us; the launch traced here: 68 us
  Pallas kernels  60.4 us (89%)
  matrix products  4.69 us (7%)
  local copies, waits for them, and re-layouts  2.81 us (4%)
    pallas_call x1, Pallas kernels, summed_products(): pl.pallas_call(gram_and_project, out_shape=jax.ShapeDtypeStruct((STREAMS,...  44 us
    pallas_call x1, Pallas kernels, factor_inverse(): pl.pallas_call(functools.partial(factor_kernel, scale), out_shape=jax.Sha...  16.5 us
    dot_general x1, matrix products, local(): lax.dot_general(stacked, inverse, (((1,), (1,)), ((), ())), precision=lax...  4.69 us
    unnamed x4, local copies, waits for them, and re-layouts  2.81 us

profile of v1, /device:TPU:1, one launch (start us, length us, event | category | flops | bytes accessed | tf_op | source)
XLA Modules:
  0.0 68.0 jit_solution(11481499326126532547)
XLA Ops:
  0.0 0.0 copy-start
  0.0 1.6 %copy-done = f32[2048,256]{1,0:T(8,128)S(1)} copy-done((f32[2048,256]{1,0:T(8,128)S(1)}, f32[2048,256]{1,0:T(8,128)}, u32[]{:S(2)}) %copy-start) | copy-done | bytes 2097176
  1.6 0.0 copy-start.1
  1.6 1.2 %copy-done.1 = f32[2048,128]{1,0:T(8,128)S(1)} copy-done((f32[2048,128]{1,0:T(8,128)S(1)}, f32[2048,128]{1,0:T(8,128)}, u32[]{:S(2)}) %copy-start.1) | copy-done | bytes 1048600
  2.8 44.0 %summed_products.1.y_ref = f32[4,1024,128]{2,1,0:T(8,128)S(1)} custom-call(f32[2048,256]{1,0:T(8,128)S(1)} %copy-done, f32[2048,128]{1,0:T(8,128)S(1)} %copy-done.1, f32[2048,1024]{1,0:T(8,128)} %j_ref.1), custom_call_target="tpu_custom_call" | custom-call | tf_op jit(solution)/shard_map/summed_products/pallas_call | solution.py:278
  46.8 16.5 %factor_inverse.1 = f32[384,384]{1,0:T(8,128)S(1)} custom-call(f32[4,1024,128]{2,1,0:T(8,128)S(1)} %summed_products.1.y_ref), custom_call_target="tpu_custom_call" | custom-call | tf_op jit(solution)/shard_map/factor_inverse/pallas_call | solution.py:440
  63.3 4.7 %fusion = f32[2048,384]{1,0:T(8,128)} fusion(f32[384,384]{1,0:T(8,128)S(1)} %factor_inverse.1, f32[2048,128]{1,0:T(8,128)S(1)} %copy-done.1, f32[2048,256]{1,0:T(8,128)S(1)} %copy-done), kind=kOutput, calls=%fused_computation | convolution fusion | flops 1812725760 | bytes 6881280 | tf_op jit(solution)/shard_map/dot_general | solution.py:456
Async XLA Ops:
  0.0 1.6 %copy-start = (f32[2048,256]{1,0:T(8,128)S(1)}, f32[2048,256]{1,0:T(8,128)}, u32[]{:S(2)}) copy-start(f32[2048,256]{1,0:T(8,128)} %v_ref.1) | copy-start | bytes 6291460
  1.6 1.2 %copy-start.1 = (f32[2048,128]{1,0:T(8,128)S(1)}, f32[2048,128]{1,0:T(8,128)}, u32[]{:S(2)}) copy-start(f32[2048,128]{1,0:T(8,128)} %w_ref.1) | copy-start | bytes 3145732

commit v2 on v1

--- a/solution.py
+++ b/solution.py
@@ -16,6 +16,7 @@
     key=lambda at: -(min(at[0], SIDE - at[0]) + min(at[1], SIDE - at[1])),
 )
 ROWS = 1024
+VMEM_LIMIT = 55_000_000
 HALF = ROWS // 2
 PART = HALF // SIDE
 PIECE = PART // SIDE**2
@@ -167,6 +168,59 @@
     return high, (value - high.astype(jnp.float32)).astype(jnp.bfloat16)
 
 
+def mat(left, right, precision=lax.Precision.HIGHEST):
+    return jnp.dot(left, right, precision=precision, preferred_element_type=jnp.float32)
+
+
+def tmat(left, right, precision=lax.Precision.HIGHEST):
+    return lax.dot_general(
+        left,
+        right,
+        (((0,), (0,)), ((), ())),
+        precision=precision,
+        preferred_element_type=jnp.float32,
+    )
+
+
+def gram_part(y_ref, scale):
+    cut = {}
+    at = 0
+    for i in range(3):
+        for j in range(i + 1):
+            cut[i, j] = y_ref[3, at : at + 128] * scale
+            at += 128
+    s_vv = jnp.concatenate(
+        [jnp.concatenate([cut[0, 0], cut[1, 0].T], axis=1), jnp.concatenate([cut[1, 0], cut[1, 1]], axis=1)], axis=0
+    )
+    s_vw = jnp.concatenate([cut[2, 0].T, cut[2, 1].T], axis=0)
+    summed = s_vw + (s_vw - mat(s_vv, s_vw))
+    cross = tmat(summed, s_vw)
+    last = cut[2, 2] - cross - cross.T + tmat(summed, mat(s_vv, summed) + summed)
+    ident = jnp.where(
+        lax.broadcasted_iota(jnp.int32, (256, 256), 0) == lax.broadcasted_iota(jnp.int32, (256, 256), 1), 1.0, 0.0
+    ).astype(jnp.float32)
+    top = jnp.concatenate([ident, summed], axis=1)
+    low = jnp.concatenate([summed.T, last], axis=1)
+    return jnp.concatenate([top, low], axis=0)
+
+
+def nt(left, right):
+    return lax.dot_general(left, right, (((1,), (1,)), ((), ())), preferred_element_type=jnp.float32)
+
+
+def half_square(y_ref, start):
+    total = None
+    for pair in range(0, HALF, 256):
+        blocks = []
+        for t in (pair, pair + 128):
+            rows = pl.ds(pl.multiple_of(start + t, 128), 128)
+            blocks.append(jnp.concatenate([y_ref[s, rows] for s in range(3)], axis=0))
+        high, low = split2(jnp.concatenate(blocks, axis=1))
+        value = nt(high, low) + nt(low, high) + nt(high, high)
+        total = value if total is None else total + value
+    return total
+
+
 CHUNK = 512
 
 
@@ -174,7 +228,7 @@
     return jnp.dot(left, right, preferred_element_type=jnp.float32)
 
 
-def gram_and_project(v_ref, w_ref, j_ref, out_ref, s_buf, j_buf, high_t, low_t, g_acc, y_ref, z0, r0, r1, z1, r2, in_s, in_j, *sems):
+def gram_and_project(scale, v_ref, w_ref, j_ref, b_ref, out_ref, s_buf, j_buf, high_t, low_t, g_acc, y_ref, z0, r0, r1, z1, r2, in_s, in_j, *sems):
     sems = [sems[i : i + 2] for i in range(0, 12, 2)]
     links = Links()
     links.greet()
@@ -252,23 +306,27 @@
     for s in range(3):
         stage[s] = share_plane(links, s, stage[s], z0, r1, z1, r2, sems[2])
     last = []
-    stage[3], own = spread_line(links, 3, stage[3], out_ref, sems[4], sems[5])
-    last += own
+    stage[3], gram = spread_line(links, 3, stage[3], out_ref, sems[4], sems[5])
     for s in range(3):
         stage[s] = spread_plane(links, s, stage[s], z1, r2, out_ref, sems[3])
-    last += spread_core(links, 3, stage[3], out_ref, sems[5])
+    gram += spread_core(links, 3, stage[3], out_ref, sems[5])
     for s in range(3):
         stage[s], own = spread_line(links, s, stage[s], out_ref, sems[4], sems[5])
         last += own
+    for copy in gram:
+        copy.wait_recv()
+    b_ref[...] = gram_part(out_ref, scale)
     for s in range(3):
         last += spread_core(links, s, stage[s], out_ref, sems[5])
+    hess = half_square(out_ref, sides[1])
     for copy in last:
         copy.wait_recv()
+    b_ref[...] += (hess + half_square(out_ref, sides[0])) * scale
     for copy in links.sent:
         copy.wait_send()
 
 
-def summed_products(basis, new_vectors, jacobian):
+def summed_products(basis, new_vectors, jacobian, scale):
     f32, bf16, dma = jnp.float32, jnp.bfloat16, pltpu.SemaphoreType.DMA
     rows = basis.shape[0]
     joint = basis.shape[1] + new_vectors.shape[1]
@@ -276,11 +334,12 @@
     for count in (4, 3, len(PLANE), len(PLANE), 3, 4):
         sems += [dma((STREAMS, count))] * 2
     return pl.pallas_call(
-        gram_and_project,
-        out_shape=jax.ShapeDtypeStruct((STREAMS, ROWS, 128), f32),
+        functools.partial(gram_and_project, scale),
+        out_shape=jax.ShapeDtypeStruct((joint, joint), f32),
         in_specs=[pl.BlockSpec(memory_space=pltpu.HBM)] * 3,
         out_specs=pl.BlockSpec(memory_space=pltpu.VMEM),
         scratch_shapes=[
+            pltpu.VMEM((STREAMS, ROWS, 128), f32),
             pltpu.VMEM((rows, joint), f32),
             pltpu.VMEM((2, rows, HALF), f32),
             pltpu.VMEM((joint, rows), bf16),
@@ -297,84 +356,20 @@
         ]
         + sems,
         compiler_params=pltpu.CompilerParams(
-            collective_id=0, has_side_effects=True, vmem_limit_bytes=48 * 1024 * 1024
+            collective_id=0, has_side_effects=True, vmem_limit_bytes=VMEM_LIMIT
         ),
         name="summed_products",
     )(basis, new_vectors, jacobian)
 
 
-def mat(left, right, precision=lax.Precision.HIGHEST):
-    return jnp.dot(left, right, precision=precision, preferred_element_type=jnp.float32)
-
-
-def tmat(left, right, precision=lax.Precision.HIGHEST):
-    return lax.dot_general(
-        left,
-        right,
-        (((0,), (0,)), ((), ())),
-        precision=precision,
-        preferred_element_type=jnp.float32,
-    )
-
-
-LEAF = 16
+LEAF = 32
 PIECES = 8
 
 
-def nt(left, right):
-    return lax.dot_general(left, right, (((1,), (1,)), ((), ())), preferred_element_type=jnp.float32)
-
-
-def build(y_ref, scale):
-    cut = {}
-    at = 0
-    for i in range(3):
-        for j in range(i + 1):
-            cut[i, j] = y_ref[3, at : at + 128] * scale
-            at += 128
-    s_vv = jnp.concatenate(
-        [jnp.concatenate([cut[0, 0], cut[1, 0].T], axis=1), jnp.concatenate([cut[1, 0], cut[1, 1]], axis=1)], axis=0
-    )
-    s_vw = jnp.concatenate([cut[2, 0].T, cut[2, 1].T], axis=0)
-    summed = s_vw + (s_vw - mat(s_vv, s_vw))
-    cross = tmat(summed, s_vw)
-    last = cut[2, 2] - cross - cross.T + tmat(summed, mat(s_vv, summed) + summed)
-    hess = jnp.zeros((384, 384), jnp.float32)
-    for pair in range(0, 8, 2):
-        rows = [
-            jnp.concatenate([y_ref[s, 128 * t : 128 * (t + 1)] for s in range(3)], axis=0) for t in (pair, pair + 1)
-        ]
-        high, low = split2(jnp.concatenate(rows, axis=1))
-        hess = hess + (nt(high, low) + nt(low, high) + nt(high, high))
-    hess = hess * scale
-    ident = jnp.where(
-        lax.broadcasted_iota(jnp.int32, (256, 256), 0) == lax.broadcasted_iota(jnp.int32, (256, 256), 1), 1.0, 0.0
-    ).astype(jnp.float32)
-    top = jnp.concatenate([ident, summed], axis=1)
-    low = jnp.concatenate([summed.T, last], axis=1)
-    return jnp.concatenate([top, low], axis=0) + hess
-
-
-def leaf_step(a, block, step):
+def eliminate(panel, columns):
     tiles = LEAF // 8
-    width = a.shape[1]
-    first = pl.multiple_of(block * 128 + step * LEAF, LEAF)
-    base = pl.multiple_of(block * 128, 128)
+    lanes = len(panel) // tiles
     sub = lax.broadcasted_iota(jnp.int32, (8, 128), 0)
-    lane = lax.broadcasted_iota(jnp.int32, (8, 128), 1)
-    columns = {}
-    for t in range(tiles):
-        diag = a[pl.ds(first + 8 * t, 8), pl.ds(base, 128)]
-        for k in range(min(LEAF, 8 * (t + 1))):
-            at = step * LEAF + k
-            columns[k, t] = jnp.broadcast_to(diag[:, at : at + 1], (8, 128))
-    panel = {}
-    for t in range(tiles):
-        for c in range(width // 128):
-            place = lane + (128 * c - first)
-            own = (place >= 0) & (place < LEAF)
-            unit = jnp.where(place == sub + 8 * t, 1.0, 0.0)
-            panel[t, c] = jnp.where(own, unit, a[pl.ds(first + 8 * t, 8), 128 * c : 128 * (c + 1)])
     factor = [jnp.zeros((8, 128), jnp.float32) for _ in range(tiles)]
     for j in range(LEAF):
         home, row = j // 8, j % 8
@@ -397,69 +392,131 @@
                     columns[k, t] = columns[k, t] - (columns[j, t] * spread) * inverse
                 else:
                     columns[k, t] = columns[k, t] - mult[t] * spread
-        for c in range(width // 128):
+        for c in range(lanes):
             spread = jnp.broadcast_to(panel[home, c][row : row + 1], (8, 128))
             for t in range(home, tiles):
                 panel[t, c] = panel[t, c] - mult[t] * spread
-    rows = jnp.concatenate(
-        [
-            jnp.concatenate([panel[t, c] * factor[t] for c in range(width // 128)], axis=1)
-            for t in range(tiles)
+    return jnp.concatenate(
+        [jnp.concatenate([panel[t, c] * factor[t] for c in range(lanes)], axis=1) for t in range(tiles)], axis=0
+    )
+
+
+def factor_inverse(a, x):
+    width = a.shape[0]
+    tiles, lanes = LEAF // 8, width // 128
+    lane = lax.broadcasted_iota(jnp.int32, (8, 128), 1)
+    sub = lax.broadcasted_iota(jnp.int32, (8, 128), 0)
+    ahead = a[0:LEAF]
+    for first in range(0, width, LEAF):
+        block = first // 128
+        after = first + LEAF
+        panel, columns = {}, {}
+        for t in range(tiles):
+            for c in range(lanes):
+                value = ahead[8 * t : 8 * t + 8, 128 * c : 128 * (c + 1)]
+                if c == block:
+                    for k in range(min(LEAF, 8 * (t + 1))):
+                        at = first % 128 + k
+                        columns[k, t] = jnp.broadcast_to(value[:, at : at + 1], (8, 128))
+                    place = lane - first % 128
+                    unit = jnp.where(place == sub + 8 * t, 1.0, 0.0)
+                    value = jnp.where((place >= 0) & (place < LEAF), unit, value)
+                panel[t, c] = value
+        rows = eliminate(panel, columns)
+        column = lax.broadcasted_iota(jnp.int32, (LEAF, width), 1)
+        x[first:after] = jnp.where(column < after, rows, 0.0)
+        if after == width:
+            break
+        none = jnp.zeros((LEAF, width), jnp.bfloat16)
+        pick = lambda parts, order: jnp.concatenate(
+            [parts[i] for i in order] + [none[:, : parts[0].shape[1]]] * (PIECES - len(order)), axis=0
+        )
+        parts = split3(rows)
+        right = pick(parts, (0, 1, 0, 2, 0, 1))
+        low = 128 * (after // 128)
+        left = pick(tuple(part[:, low:] for part in parts), (0, 0, 1, 0, 2, 1)).T
+
+        def rest(start, stop):
+            held = a[start:stop]
+            place = lax.broadcasted_iota(jnp.int32, held.shape, 1)
+            held = jnp.where((place >= first) & (place < after), 0.0, held)
+            return held - mm(left[start - low : stop - low], right)
+
+        ahead = rest(after, after + LEAF)
+        if after + LEAF < width:
+            a[after + LEAF : width] = rest(after + LEAF, width)
+
+
+OUT_CHUNK = 512
+
+
+def merge_kernel(b_ref, v_ref, w_ref, out_ref, a, x, s_buf, o_buf, in_sems, out_sems):
+    width = v_ref.shape[1]
+    joint = s_buf.shape[1]
+    loads = (
+        pltpu.make_async_copy(v_ref, s_buf.at[:, pl.ds(0, width)], in_sems.at[0]),
+        pltpu.make_async_copy(w_ref, s_buf.at[:, pl.ds(width, joint - width)], in_sems.at[1]),
+    )
+    for copy in loads:
+        copy.start()
+    a[...] = b_ref[...]
+    factor_inverse(a, x)
+    for copy in loads:
+        copy.wait()
+    high, low = split2(x[...].T)
+    edge = 256
+    both = jnp.concatenate([high[:, edge:], low[:, edge:]], axis=1)
+
+    def store(k):
+        rows = pl.ds(pl.multiple_of(k * OUT_CHUNK, OUT_CHUNK), OUT_CHUNK)
+        return pltpu.make_async_copy(o_buf.at[rows], out_ref.at[rows], out_sems.at[k])
+
+    def step(k, _):
+        rows = pl.ds(pl.multiple_of(k * OUT_CHUNK, OUT_CHUNK), OUT_CHUNK)
+        lead, trail = split2(s_buf[rows])
+        first, second = lead[:, :edge], trail[:, :edge]
+        o_buf[rows, 0:edge] = (
+            mm(first, low[:edge, :edge]) + mm(second, high[:edge, :edge]) + mm(first, high[:edge, :edge])
+        )
+        wide = mm(lead, both)
+        o_buf[rows, edge:joint] = wide[:, : joint - edge] + (wide[:, joint - edge :] + mm(trail, high[:, edge:]))
+        store(k).start()
+        return 0
+
+    chunks = s_buf.shape[0] // OUT_CHUNK
+    lax.fori_loop(0, chunks, step, 0)
+    for k in range(chunks):
+        store(k).wait()
+
+
+def merge(matrix, basis, new_vectors):
+    f32, dma = jnp.float32, pltpu.SemaphoreType.DMA
+    rows = basis.shape[0]
+    joint = basis.shape[1] + new_vectors.shape[1]
+    hbm = pl.BlockSpec(memory_space=pltpu.HBM)
+    return pl.pallas_call(
+        merge_kernel,
+        out_shape=jax.ShapeDtypeStruct((rows, joint), f32),
+        in_specs=[pl.BlockSpec(memory_space=pltpu.VMEM), hbm, hbm],
+        out_specs=hbm,
+        scratch_shapes=[
+            pltpu.VMEM((joint, joint), f32),
+            pltpu.VMEM((joint, joint), f32),
+            pltpu.VMEM((rows, joint), f32),
+            pltpu.VMEM((rows, joint), f32),
+            dma((2,)),
+            dma((rows // OUT_CHUNK,)),
         ],
-        axis=0,
-    )
-    place = lax.broadcasted_iota(jnp.int32, (LEAF, width), 1) - first
-    right = split3(rows)
-    left = split3(jnp.where(place >= LEAF, rows, 0.0))
-    none = jnp.zeros((LEAF, width), jnp.bfloat16)
-    pick = lambda parts, order: jnp.concatenate([parts[i] for i in order] + [none] * (PIECES - len(order)), axis=0)
-    update = lax.dot_general(
-        pick(left, (0, 0, 1, 0, 2, 1)),
-        pick(right, (0, 1, 0, 2, 0, 1)),
-        (((0,), (0,)), ((), ())),
-        preferred_element_type=jnp.float32,
-    )
-    place = lax.broadcasted_iota(jnp.int32, (width, width), 1) - first
-    own = (place >= 0) & (place < LEAF)
-    a[...] = jnp.where(own, 0.0, a[...]) - update
-    a[pl.ds(first, LEAF), :] = rows
-
-
-def factor_kernel(scale, y_ref, a):
-    a[...] = build(y_ref, scale)
-
-    def block_step(block, _):
-        for step in range(128 // LEAF):
-            leaf_step(a, block, step)
-        return 0
-
-    lax.fori_loop(0, a.shape[0] // 128, block_step, 0)
-
-
-def factor_inverse(summed, scale):
-    return pl.pallas_call(
-        functools.partial(factor_kernel, scale),
-        out_shape=jax.ShapeDtypeStruct((384, 384), jnp.float32),
-        in_specs=[pl.BlockSpec(memory_space=pltpu.VMEM)],
-        out_specs=pl.BlockSpec(memory_space=pltpu.VMEM),
-        compiler_params=pltpu.CompilerParams(vmem_limit_bytes=32 * 1024 * 1024),
-        name="factor_inverse",
-    )(summed)
+        compiler_params=pltpu.CompilerParams(vmem_limit_bytes=VMEM_LIMIT),
+        name="merge",
+    )(matrix, basis, new_vectors)
 
 
 def local(basis, new_vectors, jacobian):
     total = basis.shape[0] * lax.axis_size("rows") * lax.axis_size("cols")
     scale = 1.0 / total
-    stacked = jnp.concatenate([basis, new_vectors], axis=1)
-    summed = summed_products(basis, new_vectors, jacobian)
-    inverse = factor_inverse(summed, scale)
-    return lax.dot_general(
-        stacked,
-        inverse,
-        (((1,), (1,)), ((), ())),
-        precision=lax.Precision.HIGH,
-        preferred_element_type=jnp.float32,
-    )
+    matrix = summed_products(basis, new_vectors, jacobian, scale)
+    return merge(matrix, basis, new_vectors)
 
 
 def solution(mesh):

time: 68.1 us -> 61.9 us (0.909)
  matrix products: 4.69 us -> 0 us
  local copies, waits for them, and re-layouts: 2.81 us -> 0 us
  Pallas kernels: 60.4 us -> 61.6 us
    dot_general x1 -> x0, matrix products: 4.69 us -> none  [local(): lax.dot_general(stacked, inverse, (((1,), (1,)), ((), ())), precision=lax...]
    unnamed x4 -> x0, local copies, waits for them, and re-layouts: 2.81 us -> none
    pallas_call x2, Pallas kernels: 60.4 us -> 61.6 us  [the longest x1 46.4 us: summed_products(): pl.pallas_call(functools.partial(gram_and_project, scale), out_shape=jax....]
where the time goes in v2:
time: 61.9 us; the launch traced here: 61.8 us
  Pallas kernels  61.6 us (100%)
    pallas_call x1, Pallas kernels, summed_products(): pl.pallas_call(functools.partial(gram_and_project, scale), out_shape=jax....  46.4 us
    pallas_call x1, Pallas kernels, merge(): pl.pallas_call(merge_kernel, out_shape=jax.ShapeDtypeStruct((rows, joint)...  15.3 us

profile of v2, /device:TPU:1, one launch (start us, length us, event | category | flops | bytes accessed | tf_op | source)
XLA Modules:
  0.0 61.8 jit_solution(11557356087188242022)
XLA Ops:
  0.0 46.4 %summed_products.1.b_ref = f32[384,384]{1,0:T(8,128)S(1)} custom-call(f32[2048,256]{1,0:T(8,128)} %v_ref.3, f32[2048,128]{1,0:T(8,128)} %w_ref.3, f32[2048,1024]{1,0:T(8,128)} %j_ref.1), custom_call_target="tpu_custom_call" | custom-call | tf_op jit(solution)/shard_map/summed_products/pallas_call | solution.py:336
  46.4 15.3 %merge.1 = f32[2048,384]{1,0:T(8,128)} custom-call(f32[384,384]{1,0:T(8,128)S(1)} %summed_products.1.b_ref, f32[2048,256]{1,0:T(8,128)} %v_ref.3, f32[2048,128]{1,0:T(8,128)} %w_ref.3), custom_call_target="tpu_custom_call" | custom-call | tf_op jit(solution)/shard_map/merge/pallas_call | solution.py:497
